TPU v7x, 128 devices: a whole 4x4x4 slice. The times are simulated.
128 devices in a mesh: data: 1, pair: 128 (over z, y, x, core).
Axes of the slice: x: 4, y: 4, z: 4, core: 2. Of those that a mesh axis runs over, the one named last changes fastest.
Arguments:
- x_enc: bfloat16 [2048, 256, 512], P(('data', 'pair'))
- enc_len: int32 [2048], P(('data', 'pair'))
- y_dec: bfloat16 [2048, 32, 512], P(('data', 'pair'))
- enc_wq: bfloat16 [2, 512, 512], replicated
- enc_wk: bfloat16 [2, 512, 512], replicated
- enc_wv: bfloat16 [2, 512, 512], replicated
- enc_wo: bfloat16 [2, 8, 64, 512], replicated
- enc_w1: bfloat16 [2, 512, 2048], replicated
- enc_w2: bfloat16 [2, 2048, 512], replicated
- dec_wq: bfloat16 [2, 512, 512], replicated
- dec_wk: bfloat16 [2, 512, 512], replicated
- dec_wv: bfloat16 [2, 512, 512], replicated
- dec_wo: bfloat16 [2, 8, 64, 512], replicated
- crs_wq: bfloat16 [2, 512, 512], replicated
- crs_wk: bfloat16 [2, 512, 512], replicated
- crs_wv: bfloat16 [2, 512, 512], replicated
- crs_wo: bfloat16 [2, 8, 64, 512], replicated
- dec_w1: bfloat16 [2, 512, 2048], replicated
- dec_w2: bfloat16 [2, 2048, 512], replicated
Outputs:
- output: bfloat16 [2048, 32, 512], P(('data', 'pair'))
All inputs are finite; a program needn't handle non-finite values.
Results may differ from a plain program's by a relative error of at most 0.0110627.
Values are sent between devices in bfloat16 or wider.
A program may use at most 1 GiB of HBM per device.

v0:
```python
import jax
import jax.numpy as jnp
from jax import lax
from jax.sharding import PartitionSpec as P


def rms_norm(hidden):
    x_wide = hidden.astype(jnp.float32)
    inv_rms = lax.rsqrt(jnp.mean(x_wide * x_wide, axis=-1, keepdims=True) + 1e-6)
    return (x_wide * inv_rms).astype(jnp.bfloat16)


def project(source, weight):
    return jnp.dot(source, weight, preferred_element_type=jnp.float32).astype(jnp.bfloat16)


def add_to(hidden, update):
    return (hidden.astype(jnp.float32) + update).astype(jnp.bfloat16)


def key_mask(lengths, k_len):
    return (jnp.arange(k_len)[None, :] < lengths[:, None])[:, None, None, None, :]


def attend(query_rows, key_rows, value_rows, allowed, out_weight):
    num_heads, head_dim, d_model = out_weight.shape
    batch_rows, q_len = query_rows.shape[0], query_rows.shape[1]
    k_len = key_rows.shape[1]
    kv_heads = key_rows.shape[2] // head_dim
    q_per_kv = num_heads // kv_heads
    q_heads = query_rows.reshape(batch_rows, q_len, kv_heads, q_per_kv, head_dim)
    k_heads = key_rows.reshape(batch_rows, k_len, kv_heads, head_dim)
    v_heads = value_rows.reshape(batch_rows, k_len, kv_heads, head_dim)
    scores = jnp.einsum("bskrh,btkh->bkrst", q_heads, k_heads, preferred_element_type=jnp.float32) * head_dim ** -0.5
    scores = jnp.where(allowed, scores, -1e30)
    attn_probs = jax.nn.softmax(scores, axis=-1).astype(jnp.bfloat16)
    context = jnp.einsum("bkrst,btkh->bkrsh", attn_probs, v_heads, preferred_element_type=jnp.float32).astype(jnp.bfloat16)
    w_out = out_weight.reshape(kv_heads, q_per_kv, head_dim, d_model)
    return jnp.einsum("bkrsh,krhd->bsd", context, w_out, preferred_element_type=jnp.float32)


def feed_forward(hidden, w_up, w_down):
    normed = rms_norm(hidden)
    inner_act = jax.nn.gelu(jnp.dot(normed, w_up, preferred_element_type=jnp.float32)).astype(jnp.bfloat16)
    return add_to(hidden, jnp.dot(inner_act, w_down, preferred_element_type=jnp.float32))


def encode(x_enc, enc_len, enc_weights):
    enc_wq, enc_wk, enc_wv, enc_wo, enc_w1, enc_w2 = enc_weights
    allowed = key_mask(enc_len, x_enc.shape[1])
    hidden = x_enc
    for layer_idx in range(enc_wq.shape[0]):
        normed = rms_norm(hidden)
        attn_out = attend(project(normed, enc_wq[layer_idx]), project(normed, enc_wk[layer_idx]), project(normed, enc_wv[layer_idx]), allowed, enc_wo[layer_idx])
        hidden = feed_forward(add_to(hidden, attn_out), enc_w1[layer_idx], enc_w2[layer_idx])
    return rms_norm(hidden)


def decode(y_dec, cross_keys, cross_vals, partner_len, dec_weights):
    dec_wq, dec_wk, dec_wv, dec_wo, crs_wq, crs_wo, dec_w1, dec_w2 = dec_weights
    dec_len = y_dec.shape[1]
    causal = jnp.arange(dec_len)[:, None] >= jnp.arange(dec_len)[None, :]
    cross_ok = key_mask(partner_len, cross_keys[0].shape[1])
    hidden = y_dec
    for layer_idx in range(dec_wq.shape[0]):
        normed = rms_norm(hidden)
        self_out = attend(project(normed, dec_wq[layer_idx]), project(normed, dec_wk[layer_idx]), project(normed, dec_wv[layer_idx]), causal, dec_wo[layer_idx])
        hidden = add_to(hidden, self_out)
        cross_out = attend(project(rms_norm(hidden), crs_wq[layer_idx]), cross_keys[layer_idx], cross_vals[layer_idx], cross_ok, crs_wo[layer_idx])
        hidden = feed_forward(add_to(hidden, cross_out), dec_w1[layer_idx], dec_w2[layer_idx])
    return hidden


def solution(mesh):
    pair_size = mesh.shape["pair"]
    to_partner = [(source, (source + pair_size // 2) % pair_size) for source in range(pair_size)]
    row_spec = P(("data", "pair"))
    full_spec = P()

    def per_device(x_enc, enc_len, y_dec, enc_wq, enc_wk, enc_wv, enc_wo, enc_w1, enc_w2, dec_wq, dec_wk, dec_wv, dec_wo, crs_wq, crs_wk, crs_wv, crs_wo, dec_w1, dec_w2):
        enc_out = encode(x_enc, enc_len, (enc_wq, enc_wk, enc_wv, enc_wo, enc_w1, enc_w2))
        own_keys = [project(enc_out, crs_wk[layer_idx]) for layer_idx in range(crs_wk.shape[0])]
        own_vals = [project(enc_out, crs_wv[layer_idx]) for layer_idx in range(crs_wv.shape[0])]
        cross_keys, cross_vals, partner_len = lax.ppermute((own_keys, own_vals, enc_len), "pair", to_partner)
        return decode(y_dec, cross_keys, cross_vals, partner_len, (dec_wq, dec_wk, dec_wv, dec_wo, crs_wq, crs_wo, dec_w1, dec_w2))

    return jax.shard_map(per_device, mesh=mesh, in_specs=(row_spec, row_spec, row_spec) + (full_spec,) * 16, out_specs=row_spec, check_vma=False)
```

profile of v0, /device:TPU:0, one launch (start us, length us, event | category | flops | bytes accessed | tf_op | source)
XLA Modules:
  0.0 630.8 jit_solution(14456375357651737593)
XLA Ops:
  0.0 4.0 collective-permute-start
  4.8 3.1 fusion.28
  7.9 5.0 fusion.114
  12.9 6.5 %copy.34 = bf16[16,256,512]{1,2,0:T(8,128)(2,1)} copy(bf16[16,256,512]{2,1,0:T(8,128)(2,1)} %fusion.114) | data formatting | bytes 8388608 | tf_op jit(solution)/shard_map/convert_element_type | solution.py:14
  19.4 6.5 %fusion.117 = bf16[16,256,512]{2,1,0:T(8,128)(2,1)} fusion(bf16[16,256,512]{2,1,0:T(8,128)(2,1)} %param.19, f32[16,256]{1,0:T(8,128)S(1)} %add_rsqrt_fusion.4, bf16[2,512,512]{2,1,0:T(8,128)(2,1)S(1)} %copy-done.4), kind=kOutput, calls=%fused_computation.117 | convolution fusion | flops 2155872256 | bytes 8929280 | tf_op jit(solution)/shard_map/dot_general | solution.py:14
  25.9 6.5 %copy.35 = bf16[16,256,512]{1,2,0:T(8,128)(2,1)} copy(bf16[16,256,512]{2,1,0:T(8,128)(2,1)} %fusion.117) | data formatting | bytes 8388608 | tf_op jit(solution)/shard_map/convert_element_type | solution.py:14
  32.4 6.5 %fusion.120 = bf16[16,256,512]{2,1,0:T(8,128)(2,1)} fusion(bf16[16,256,512]{2,1,0:T(8,128)(2,1)} %param.19, f32[16,256]{1,0:T(8,128)S(1)} %add_rsqrt_fusion.4, bf16[2,512,512]{2,1,0:T(8,128)(2,1)S(1)} %copy-done.6), kind=kOutput, calls=%fused_computation.118 | convolution fusion | flops 2155872256 | bytes 8929280 | tf_op jit(solution)/shard_map/dot_general | solution.py:14
  38.9 6.4 %copy.36 = bf16[16,256,512]{1,2,0:T(8,128)(2,1)} copy(bf16[16,256,512]{2,1,0:T(8,128)(2,1)} %fusion.120) | data formatting | bytes 8388608 | tf_op jit(solution)/shard_map/convert_element_type | solution.py:14
  45.3 17.4 %bitcast_reduce_fusion.1 = (f32[16,8,256]{2,1,0:T(8,128)S(1)}, f32[16,8,256,256]{3,2,1,0:T(8,128)}) fusion(pred[16,256]{1,0:T(8,128)(4,1)S(1)} %iota_compare_fusion, bf16[16,256,8,64]{1,3,2,0:T(8,128)(2,1)} %bitcast.436, bf16[16,256,8,64]{1,3,2,0:T(8,128)(2,1)} %bitcast.437), kind=kOutput, calls=%fused_computation.23 | convolution fusion | flops 1098874880 | bytes 42078208 | tf_op jit(solution)/shard_map/bskrh,btkh->bkrst/dot_general | solution.py:34
  62.7 14.9 %fusion.18 = f32[16,8,256]{2,1,0:T(8,128)S(1)} fusion(f32[16,8,256,256]{3,2,1,0:T(8,128)} %get-tuple-element.8, f32[16,8,256]{2,1,0:T(8,128)S(1)} %get-tuple-element.7, pred[16,256]{1,0:T(8,128)(4,1)S(1)} %iota_compare_fusion), kind=kLoop, calls=%fused_computation.28 | loop fusion | flops 33521664 | bytes 33820672 | tf_op jit(solution)/shard_map/reduce_sum | solution.py:36
  77.6 18.7 %fusion.31 = (f32[16,256]{1,0:T(8,128)S(1)}, bf16[16,256,512]{2,1,0:T(8,128)(2,1)}) fusion(bf16[2,8,64,512]{3,2,1,0:T(8,128)(2,1)S(1)} %copy-done.7, bf16[16,256,8,64]{1,3,2,0:T(8,128)(2,1)} %bitcast.443, f32[16,8,256]{2,1,0:T(8,128)S(1)} %fusion.18, f32[16,8,256]{2,1,0:T(8,128)S(1)} %get-tuple-element.7, f32[16,8,256,256]{3,2,1,0:T(8,128)} %get-tuple-element.8, ...), kind=kOutput, calls=%fused_computation.55 | convolution fusion | flops 3277844480 | bytes 46944256 | tf_op jit(solution)/shard_map/bkrsh,krhd->bsd/dot_general | solution.py:39
  96.3 35.7 %fusion.34 = (f32[16,256]{1,0:T(8,128)S(1)}, bf16[16,256,512]{2,1,0:T(8,128)(2,1)}) fusion(bf16[2,2048,512]{2,1,0:T(8,128)(2,1)} %param.27, bf16[16,256,512]{2,1,0:T(8,128)(2,1)} %get-tuple-element.10, f32[16,256]{1,0:T(8,128)S(1)} %add_rsqrt_fusion.3, bf16[2,512,2048]{2,1,0:T(8,128)(2,1)} %param.26), kind=kOutput, calls=%fused_computation.58 | convolution fusion | flops 17274236928 | bytes 16809984 | tf_op jit(solution)/shard_map/dot_general | solution.py:45
  132.1 6.7 %fusion.126 = bf16[16,256,512]{2,1,0:T(8,128)(2,1)} fusion(bf16[16,256,512]{2,1,0:T(8,128)(2,1)} %get-tuple-element.12, f32[16,256]{1,0:T(8,128)S(1)} %add_rsqrt_fusion.2, bf16[2,512,512]{2,1,0:T(8,128)(2,1)S(1)} %copy-done.4), kind=kOutput, calls=%fused_computation.120 | convolution fusion | flops 2155872256 | bytes 8929280 | tf_op jit(solution)/shard_map/dot_general | solution.py:14
  138.8 4.0 fusion.123
  142.8 4.0 fusion.129
  146.7 6.4 %copy.38 = bf16[16,256,512]{1,2,0:T(8,128)(2,1)} copy(bf16[16,256,512]{2,1,0:T(8,128)(2,1)} %fusion.126) | data formatting | bytes 8388608 | tf_op jit(solution)/shard_map/convert_element_type | solution.py:14
  153.1 6.4 %copy.37 = bf16[16,256,512]{1,2,0:T(8,128)(2,1)} copy(bf16[16,256,512]{2,1,0:T(8,128)(2,1)} %fusion.123) | data formatting | bytes 8388608 | tf_op jit(solution)/shard_map/convert_element_type | solution.py:14
  159.5 6.4 %copy.39 = bf16[16,256,512]{1,2,0:T(8,128)(2,1)} copy(bf16[16,256,512]{2,1,0:T(8,128)(2,1)} %fusion.129) | data formatting | bytes 8388608 | tf_op jit(solution)/shard_map/convert_element_type | solution.py:14
  165.9 17.4 %bitcast_reduce_fusion = (f32[16,8,256]{2,1,0:T(8,128)S(1)}, f32[16,8,256,256]{3,2,1,0:T(8,128)}) fusion(pred[16,256]{1,0:T(8,128)(4,1)S(1)} %iota_compare_fusion, bf16[16,256,8,64]{1,3,2,0:T(8,128)(2,1)} %bitcast.439, bf16[16,256,8,64]{1,3,2,0:T(8,128)(2,1)} %bitcast.438), kind=kOutput, calls=%fused_computation.19 | convolution fusion | flops 1098874880 | bytes 42078208 | tf_op jit(solution)/shard_map/bskrh,btkh->bkrst/dot_general | solution.py:34
  183.3 14.8 %fusion.19 = f32[16,8,256]{2,1,0:T(8,128)S(1)} fusion(f32[16,8,256,256]{3,2,1,0:T(8,128)} %get-tuple-element.14, f32[16,8,256]{2,1,0:T(8,128)S(1)} %get-tuple-element.13, pred[16,256]{1,0:T(8,128)(4,1)S(1)} %iota_compare_fusion), kind=kLoop, calls=%fused_computation.29 | loop fusion | flops 33521664 | bytes 33820672 | tf_op jit(solution)/shard_map/reduce_sum | solution.py:36
  198.1 18.4 %fusion.37 = (f32[16,256]{1,0:T(8,128)S(1)}, bf16[16,256,512]{2,1,0:T(8,128)(2,1)}) fusion(bf16[2,8,64,512]{3,2,1,0:T(8,128)(2,1)S(1)} %copy-done.7, bf16[16,256,8,64]{1,3,2,0:T(8,128)(2,1)} %bitcast.442, f32[16,8,256]{2,1,0:T(8,128)S(1)} %fusion.19, f32[16,8,256]{2,1,0:T(8,128)S(1)} %get-tuple-element.13, f32[16,8,256,256]{3,2,1,0:T(8,128)} %get-tuple-element.14, ...), kind=kOutput, calls=%fused_computation.61 | convolution fusion | flops 3277844480 | bytes 46944256 | tf_op jit(solution)/shard_map/bkrsh,krhd->bsd/dot_general | solution.py:39
  216.6 27.0 %fusion.26 = (f32[16,256]{1,0:T(8,128)S(1)}, bf16[16,256,512]{2,1,0:T(8,128)(2,1)}) fusion(bf16[2,2048,512]{2,1,0:T(8,128)(2,1)} %param.27, bf16[16,256,512]{2,1,0:T(8,128)(2,1)} %get-tuple-element.16, f32[16,256]{1,0:T(8,128)S(1)} %add_rsqrt_fusion.1, bf16[2,512,2048]{2,1,0:T(8,128)(2,1)} %param.26), kind=kOutput, calls=%fused_computation.50 | convolution fusion | flops 17274236928 | bytes 16809984 | tf_op jit(solution)/shard_map/dot_general | solution.py:45
  243.6 6.7 %fusion.102 = bf16[16,256,512]{2,1,0:T(8,128)(2,1)} fusion(bf16[16,256,512]{2,1,0:T(8,128)(2,1)} %get-tuple-element.18, f32[16,256]{1,0:T(8,128)S(1)} %add_rsqrt_fusion, bf16[2,512,512]{2,1,0:T(8,128)(2,1)S(1)} %copy-done.8), kind=kOutput, calls=%fused_computation.112 | convolution fusion | flops 2155872256 | bytes 8929280 | tf_op jit(solution)/shard_map/dot_general | solution.py:14
  250.6 4.0 fusion.105
  254.6 3.2 collective-permute-start.2
  257.8 3.9 fusion.108
  262.1 4.0 fusion.111
  266.0 3.2 collective-permute-start.4
  276.6 1.9 fusion.342
  279.1 2.6 fusion.210
  284.6 60.7 %collective-permute-done.1 = bf16[16,256,512]{2,1,0:T(8,128)(2,1)} collective-permute-done((bf16[16,256,512]{2,1,0:T(8,128)(2,1)}, bf16[16,256,512]{2,1,0:T(8,128)(2,1)}, u32[]{:S(2)}, u32[]{:S(2)}) %collective-permute-start.1) | collective-permute-done | bytes 4194336 | tf_op jit(solution)/shard_map/ppermute | solution.py:84
  345.2 6.6 %copy.40 = bf16[16,256,512]{1,2,0:T(8,128)(2,1)} copy(bf16[16,256,512]{2,1,0:T(8,128)(2,1)} %collective-permute-done.1) | data formatting | bytes 8388608 | tf_op jit(solution)/shard_map/ppermute | solution.py:84
  351.8 3.1 bitcast_reduce_fusion.3
  355.0 2.0 copy-done.1
  358.4 76.7 %collective-permute-done.2 = bf16[16,256,512]{2,1,0:T(8,128)(2,1)} collective-permute-done((bf16[16,256,512]{2,1,0:T(8,128)(2,1)}, bf16[16,256,512]{2,1,0:T(8,128)(2,1)}, u32[]{:S(2)}, u32[]{:S(2)}) %collective-permute-start.2) | collective-permute-done | bytes 4194336 | tf_op jit(solution)/shard_map/ppermute | solution.py:84
  435.1 6.4 %copy.42 = bf16[16,256,512]{1,2,0:T(8,128)(2,1)} copy(bf16[16,256,512]{2,1,0:T(8,128)(2,1)} %collective-permute-done.2) | data formatting | bytes 8388608 | tf_op jit(solution)/shard_map/ppermute | solution.py:84
  441.5 5.2 fusion.212
  446.7 6.1 fusion.214
  461.1 2.2 fusion.365
  464.0 3.1 fusion.216
  469.3 55.7 %collective-permute-done.3 = bf16[16,256,512]{2,1,0:T(8,128)(2,1)} collective-permute-done((bf16[16,256,512]{2,1,0:T(8,128)(2,1)}, bf16[16,256,512]{2,1,0:T(8,128)(2,1)}, u32[]{:S(2)}, u32[]{:S(2)}) %collective-permute-start.3) | collective-permute-done | bytes 4194336 | tf_op jit(solution)/shard_map/ppermute | solution.py:84
  525.0 6.6 %copy.45 = bf16[16,256,512]{1,2,0:T(8,128)(2,1)} copy(bf16[16,256,512]{2,1,0:T(8,128)(2,1)} %collective-permute-done.3) | data formatting | bytes 8388608 | tf_op jit(solution)/shard_map/ppermute | solution.py:84
  531.6 3.1 bitcast_reduce_fusion.2
  534.8 2.0 copy-done
  538.2 75.4 %collective-permute-done.4 = bf16[16,256,512]{2,1,0:T(8,128)(2,1)} collective-permute-done((bf16[16,256,512]{2,1,0:T(8,128)(2,1)}, bf16[16,256,512]{2,1,0:T(8,128)(2,1)}, u32[]{:S(2)}, u32[]{:S(2)}) %collective-permute-start.4) | collective-permute-done | bytes 4194336 | tf_op jit(solution)/shard_map/ppermute | solution.py:84
  613.7 6.4 %copy.47 = bf16[16,256,512]{1,2,0:T(8,128)(2,1)} copy(bf16[16,256,512]{2,1,0:T(8,128)(2,1)} %collective-permute-done.4) | data formatting | bytes 8388608 | tf_op jit(solution)/shard_map/ppermute | solution.py:84
  620.1 4.6 fusion.218
  624.7 5.7 fusion.201
  (74 shorter events, 26.3 us)
Async XLA Ops:
  0.0 7.9 %copy-start.2 = (bf16[16,256,512]{2,1,0:T(8,128)(2,1)S(1)}, bf16[16,256,512]{2,1,0:T(8,128)(2,1)}, u32[]{:S(2)}) copy-start(bf16[16,256,512]{2,1,0:T(8,128)(2,1)} %param.19) | copy-start | bytes 12582916
  0.0 283.8 %collective-permute-start = (s32[16]{0:T(128)}, s32[16]{0:T(128)}, u32[]{:S(2)}, u32[]{:S(2)}) collective-permute-start(s32[16]{0:T(128)} %param.20), channel_id=1, source_target_pairs={{0,64},{1,65},{2,66},{3,67},{4,68},{5,69},{6,70},{7,71},{8,72},{9,... | collective-permute-start | bytes 200 | tf_op jit(solution)/shard_map/ppermute | solution.py:84
  12.9 6.5 %copy-start.4 = (bf16[2,512,512]{2,1,0:T(8,128)(2,1)S(1)}, bf16[2,512,512]{2,1,0:T(8,128)(2,1)}, u32[]{:S(2)}) copy-start(bf16[2,512,512]{2,1,0:T(8,128)(2,1)} %param.22) | copy-start | bytes 3145732
  25.9 6.5 %copy-start.6 = (bf16[2,512,512]{2,1,0:T(8,128)(2,1)S(1)}, bf16[2,512,512]{2,1,0:T(8,128)(2,1)}, u32[]{:S(2)}) copy-start(bf16[2,512,512]{2,1,0:T(8,128)(2,1)} %param.24) | copy-start | bytes 3145732
  62.7 14.9 %copy-start.7 = (bf16[2,8,64,512]{3,2,1,0:T(8,128)(2,1)S(1)}, bf16[2,8,64,512]{3,2,1,0:T(8,128)(2,1)}, u32[]{:S(2)}) copy-start(bf16[2,8,64,512]{3,2,1,0:T(8,128)(2,1)} %param.25) | copy-start | bytes 3145732
  132.1 6.7 %copy-start.5 = (bf16[2,512,512]{2,1,0:T(8,128)(2,1)S(1)}, bf16[2,512,512]{2,1,0:T(8,128)(2,1)}, u32[]{:S(2)}) copy-start(bf16[2,512,512]{2,1,0:T(8,128)(2,1)} %param.23) | copy-start | bytes 3145732
  132.1 6.7 %copy-start.17 = (bf16[16,256,512]{2,1,0:T(8,128)(2,1)S(1)}, bf16[16,256,512]{2,1,0:T(8,128)(2,1)}, u32[]{:S(2)}) copy-start(bf16[16,256,512]{2,1,0:T(8,128)(2,1)} %get-tuple-element.12) | copy-start | bytes 12582916
  216.6 27.0 %copy-start.8 = (bf16[2,512,512]{2,1,0:T(8,128)(2,1)S(1)}, bf16[2,512,512]{2,1,0:T(8,128)(2,1)}, u32[]{:S(2)}) copy-start(bf16[2,512,512]{2,1,0:T(8,128)(2,1)} %param.33) | copy-start | bytes 3145732
  243.6 7.0 %copy-start.9 = (bf16[2,512,512]{2,1,0:T(8,128)(2,1)S(1)}, bf16[2,512,512]{2,1,0:T(8,128)(2,1)}, u32[]{:S(2)}) copy-start(bf16[2,512,512]{2,1,0:T(8,128)(2,1)} %param.34) | copy-start | bytes 3145732
  243.6 7.0 %copy-start.18 = (bf16[16,256,512]{2,1,0:T(8,128)(2,1)S(1)}, bf16[16,256,512]{2,1,0:T(8,128)(2,1)}, u32[]{:S(2)}) copy-start(bf16[16,256,512]{2,1,0:T(8,128)(2,1)} %get-tuple-element.18) | copy-start | bytes 12582916
  250.3 95.0 %collective-permute-start.1 = (bf16[16,256,512]{2,1,0:T(8,128)(2,1)}, bf16[16,256,512]{2,1,0:T(8,128)(2,1)}, u32[]{:S(2)}, u32[]{:S(2)}) collective-permute-start(bf16[16,256,512]{2,1,0:T(8,128)(2,1)} %fusion.102), channel_id=1, source_target_pairs={{0,64},{1,65},{2,66},{3,67},{4,68},{5,69},{6,70},{7,71},{8,72},{9,... | collective-permute-start | bytes 12582920 | tf_op jit(solution)/shard_map/ppermute | solution.py:84
  254.6 180.5 %collective-permute-start.2 = (bf16[16,256,512]{2,1,0:T(8,128)(2,1)}, bf16[16,256,512]{2,1,0:T(8,128)(2,1)}, u32[]{:S(2)}, u32[]{:S(2)}) collective-permute-start(bf16[16,256,512]{2,1,0:T(8,128)(2,1)} %fusion.105), channel_id=1, source_target_pairs={{0,64},{1,65},{2,66},{3,67},{4,68},{5,69},{6,70},{7,71},{8,72},{9,... | collective-permute-start | bytes 12582920 | tf_op jit(solution)/shard_map/ppermute | solution.py:84
  261.7 7.5 %copy-start.3 = (bf16[16,32,512]{2,1,0:T(8,128)(2,1)S(1)}, bf16[16,32,512]{2,1,0:T(8,128)(2,1)}, u32[]{:S(2)}) copy-start(bf16[16,32,512]{2,1,0:T(8,128)(2,1)} %param.21) | copy-start | bytes 1572868
  261.7 7.7 %copy-start.10 = (bf16[2,512,512]{2,1,0:T(8,128)(2,1)S(1)}, bf16[2,512,512]{2,1,0:T(8,128)(2,1)}, u32[]{:S(2)}) copy-start(bf16[2,512,512]{2,1,0:T(8,128)(2,1)} %param.29) | copy-start | bytes 3145732
  261.7 263.3 %collective-permute-start.3 = (bf16[16,256,512]{2,1,0:T(8,128)(2,1)}, bf16[16,256,512]{2,1,0:T(8,128)(2,1)}, u32[]{:S(2)}, u32[]{:S(2)}) collective-permute-start(bf16[16,256,512]{2,1,0:T(8,128)(2,1)} %fusion.108), channel_id=1, source_target_pairs={{0,64},{1,65},{2,66},{3,67},{4,68},{5,69},{6,70},{7,71},{8,72},{9,... | collective-permute-start | bytes 12582920 | tf_op jit(solution)/shard_map/ppermute | solution.py:84
  266.0 347.7 %collective-permute-start.4 = (bf16[16,256,512]{2,1,0:T(8,128)(2,1)}, bf16[16,256,512]{2,1,0:T(8,128)(2,1)}, u32[]{:S(2)}, u32[]{:S(2)}) collective-permute-start(bf16[16,256,512]{2,1,0:T(8,128)(2,1)} %fusion.111), channel_id=1, source_target_pairs={{0,64},{1,65},{2,66},{3,67},{4,68},{5,69},{6,70},{7,71},{8,72},{9,... | collective-permute-start | bytes 12582920 | tf_op jit(solution)/shard_map/ppermute | solution.py:84
  355.0 2.0 copy-start.1
  358.4 83.1 %copy-start.13 = (bf16[2,8,64,512]{3,2,1,0:T(8,128)(2,1)S(1)}, bf16[2,8,64,512]{3,2,1,0:T(8,128)(2,1)}, u32[]{:S(2)}) copy-start(bf16[2,8,64,512]{3,2,1,0:T(8,128)(2,1)} %param.35) | copy-start | bytes 3145732
  446.7 6.1 copy-start.11
  446.7 9.2 %copy-start.12 = (bf16[2,512,512]{2,1,0:T(8,128)(2,1)S(1)}, bf16[2,512,512]{2,1,0:T(8,128)(2,1)}, u32[]{:S(2)}) copy-start(bf16[2,512,512]{2,1,0:T(8,128)(2,1)} %param.28) | copy-start | bytes 3145732
  454.4 4.7 copy-start.16
  534.8 2.0 copy-start
  538.2 81.9 %copy-start.14 = (bf16[2,8,64,512]{3,2,1,0:T(8,128)(2,1)S(1)}, bf16[2,8,64,512]{3,2,1,0:T(8,128)(2,1)}, u32[]{:S(2)}) copy-start(bf16[2,8,64,512]{3,2,1,0:T(8,128)(2,1)} %param.35) | copy-start | bytes 3145732
  538.2 81.9 %copy-start.15 = (bf16[16,32,512]{2,1,0:T(8,128)(2,1)S(1)}, bf16[16,32,512]{2,1,0:T(8,128)(2,1)}, u32[]{:S(2)}) copy-start(bf16[16,32,512]{2,1,0:T(8,128)(2,1)} %get-tuple-element.30) | copy-start | bytes 1572868
where the time goes:
time: 642 us; the launch traced here: 631 us
  waiting for transfers between devices  268 us (42%)
  matrix products  235 us (37%)
  local copies, waits for them, and re-layouts  76.8 us (12%)
  other arithmetic  38.7 us (6%)
  starting transfers between devices  11.1 us (2%)
    ppermute x5, waiting for transfers between devices, per_device(): lax.ppermute((own_keys, own_vals, enc_len), 'pair', to_partner)  268 us
    dot_general x4, matrix products, feed_forward(): jnp.dot(inner_act, w_down, preferred_element_type=jnp.float32)  74.4 us
    dot_general x18, matrix products, project(): jnp.dot(source, weight, preferred_element_type=jnp.float32)  62.5 us
    dot_general x6, matrix products, attend(): jnp.einsum('bkrsh,krhd->bsd', context, w_out, preferred_element_type=jnp....  52.7 us
    dot_general x6, matrix products, attend(): jnp.einsum('bskrh,btkh->bkrst', q_heads, k_heads, preferred_element_type=...  45.2 us
    convert_element_type x6, local copies, waits for them, and re-layouts, project(): jnp.dot(source, weight, preferred_element_type=jnp.float32)  38.5 us
    reduce_sum x6, other arithmetic, attend(): attn_probs = jax.nn.softmax(scores, axis=-1).astype(jnp.bfloat16)  33.9 us
    ppermute x4, local copies, waits for them, and re-layouts, per_device(): lax.ppermute((own_keys, own_vals, enc_len), 'pair', to_partner)  26 us
  transfers between devices with their start and end apart: 5, of which 4 were waited for; matrix products, arithmetic and copies ran while one was open for 52% of the time, Pallas kernels for 0%

commit v1 on v0

v1 whole, which is shorter than its diff:
```python
import functools

import jax
import jax.numpy as jnp
from jax import lax
from jax.experimental import pallas as pl
from jax.experimental.pallas import tpu as pltpu
from jax.sharding import PartitionSpec as P

BF = jnp.bfloat16
F32 = jnp.float32
BLK = 256
GRAN = 16
HD = 64
LOG2E = 1.4426950408889634
NEG = -1e30


def dot(a, b):
    return jnp.dot(a, b, preferred_element_type=F32)


def dot_t(a, b):
    return lax.dot_general(a, b, (((1,), (1,)), ((), ())), preferred_element_type=F32)


def norm(x):
    xw = x.astype(F32)
    return (xw * lax.rsqrt(jnp.mean(xw * xw, axis=-1, keepdims=True) + 1e-6)).astype(BF)


def gelu(x):
    inner = x * (0.7978845608028654 + 0.035677408136300125 * (x * x))
    half = 0.5 * x
    return half + half * jnp.tanh(inner)


def ffn(h1, w1_ref, w2_ref, layer, u_ref):
    hn = norm(h1)
    ff = w1_ref.shape[2]
    for c in range(0, ff, 512):
        u_ref[:, c:c + 512] = gelu(dot(hn, w1_ref[layer, :, c:c + 512])).astype(BF)
    return (h1.astype(F32) + dot(u_ref[...], w2_ref[layer])).astype(BF)


def head_attention(keys, queries, vtx_ref, ctx_ref, mask=None):
    lk, lq = keys.shape[0], queries.shape[0]
    heads = keys.shape[1] // HD
    lane = lax.broadcasted_iota(jnp.int32, (lq, 2 * HD), 1)
    for h in range(heads):
        pair = slice(128 * (h // 2), 128 * (h // 2) + 128)
        mine = (lane < HD) if h % 2 == 0 else (lane >= HD)
        q = jnp.where(mine, queries[:, pair], jnp.zeros((), BF))
        s = dot_t(keys[:, pair], q)
        if mask is not None:
            s = jnp.where(mask, s, NEG)
        m = jnp.max(s, axis=0, keepdims=True)
        e = jnp.exp2((s - m) * LOG2E).astype(BF)
        o = dot(vtx_ref[h, :, :lk], e)
        ctx_ref[h * HD:(h + 1) * HD, :lq] = (o[:HD] * (1.0 / o[HD:HD + 1])).astype(BF)


def store_values(v, vtx_ref, lk):
    vt = v.T
    for h in range(v.shape[1] // HD):
        vtx_ref[h, :HD, :lk] = vt[h * HD:(h + 1) * HD]


def row_starts(len_ref, rows):
    starts = [jnp.int32(0)]
    for r in range(rows):
        starts.append(starts[-1] + (len_ref[r] + (GRAN - 1)) // GRAN * GRAN)
    return starts


def encoder_kernel(rows, seq, len_ref, x_hbm, wq_h, wk_h, wv_h, wo_h, w1_h, w2_h, cwk_h, cwv_h,
                   ck_hbm, cv_hbm,
                   h_ref, q_ref, k_ref, v_ref, c_ref, u_ref, vtx_ref, ctx_ref,
                   wq, wk, wv, wo, w1, w2, cwk, cwv, start_ref, x_sem, w_sem, o_sem):
    layers = wq.shape[0]
    x_copies = [pltpu.make_async_copy(x_hbm.at[r], q_ref.at[pl.ds(r * seq, seq)], x_sem.at[r]) for r in range(rows)]
    for copy in x_copies:
        copy.start()
    pairs = [(wq_h, wq), (wk_h, wk), (wv_h, wv), (wo_h, wo), (w1_h, w1), (w2_h, w2)]
    w_copies = {}
    for layer in range(layers):
        for i, (src, dst) in enumerate(pairs):
            w_copies[i, layer] = pltpu.make_async_copy(src.at[layer], dst.at[layer], w_sem.at[layer, i])
            w_copies[i, layer].start()
    for i, (src, dst) in enumerate([(cwk_h, cwk), (cwv_h, cwv)]):
        w_copies[6 + i, 0] = pltpu.make_async_copy(src, dst, w_sem.at[0, 6 + i])
        w_copies[6 + i, 0].start()

    starts = row_starts(len_ref, rows)
    for r in range(rows):
        start_ref[r] = starts[r]
    blocks = (starts[rows] + (BLK - 1)) // BLK
    for r in range(rows):
        x_copies[r].wait()
        h_ref[pl.ds(pl.multiple_of(starts[r], GRAN), seq)] = q_ref[pl.ds(r * seq, seq)]

    def block_at(b):
        return pl.ds(pl.multiple_of(b * BLK, BLK), BLK)

    def project(b, hidden, layer):
        hn = norm(hidden)
        at = block_at(b)
        q_ref[at] = (dot(hn, wq[layer]).astype(BF) * BF(HD ** -0.5))
        k_ref[at] = dot(hn, wk[layer]).astype(BF)
        v_ref[at] = dot(hn, wv[layer]).astype(BF)

    def attention(r, lq, lk):
        begin = pl.multiple_of(start_ref[r], GRAN)
        length = len_ref[r]
        at_k, at_q = pl.ds(begin, lk), pl.ds(begin, lq)
        inside = lax.broadcasted_iota(jnp.int32, (lk, 1), 0) < length
        keys = jnp.where(inside, k_ref[at_k], k_ref[pl.ds(begin, GRAN)][:1])
        store_values(jnp.where(inside, v_ref[at_k], jnp.zeros((), BF)), vtx_ref, lk)
        weight = (lax.broadcasted_iota(jnp.int32, (GRAN, lk), 1) < length).astype(F32).astype(BF)
        for h in range(vtx_ref.shape[0]):
            vtx_ref[h, HD:HD + GRAN, :lk] = weight
        head_attention(keys, q_ref[at_q], vtx_ref, ctx_ref)
        c_ref[at_q] = ctx_ref[:, :lq].T

    for i in range(3):
        w_copies[i, 0].wait()

    def first(b, carry):
        project(b, h_ref[block_at(b)], 0)
        return carry
    lax.fori_loop(0, blocks, first, 0)

    for layer in range(layers):
        def attend_row(r, carry):
            @pl.when(len_ref[r] <= 128)
            def _():
                attention(r, 128, 128)

            @pl.when(len_ref[r] > 128)
            def _():
                attention(r, 256, 256)
            return carry
        lax.fori_loop(0, rows, attend_row, 0)

        for i in range(3, 6):
            w_copies[i, layer].wait()
        if layer + 1 < layers:
            for i in range(3):
                w_copies[i, layer + 1].wait()
        else:
            w_copies[6, 0].wait()
            w_copies[7, 0].wait()

        def dense(b, carry):
            at = block_at(b)
            h1 = (h_ref[at].astype(F32) + dot(c_ref[at], wo[layer])).astype(BF)
            h2 = ffn(h1, w1, w2, layer, u_ref)
            if layer + 1 < layers:
                h_ref[at] = h2
                project(b, h2, layer + 1)
            else:
                out = norm(h2)
                for i, (buf, weight, dst) in enumerate([(q_ref, cwk.at[0], ck_hbm.at[0]), (k_ref, cwv.at[0], cv_hbm.at[0]),
                                                        (v_ref, cwk.at[1], ck_hbm.at[1]), (c_ref, cwv.at[1], cv_hbm.at[1])]):
                    buf[at] = dot(out, weight[...]).astype(BF)
                    pltpu.make_async_copy(buf.at[at], dst.at[at], o_sem.at[i, b]).start()
            return carry
        lax.fori_loop(0, blocks, dense, 0)

    def finish(b, carry):
        at = block_at(b)
        for i, (buf, dst) in enumerate([(q_ref, ck_hbm.at[0]), (k_ref, cv_hbm.at[0]), (v_ref, ck_hbm.at[1]), (c_ref, cv_hbm.at[1])]):
            pltpu.make_async_copy(buf.at[at], dst.at[at], o_sem.at[i, b]).wait()
        return carry
    lax.fori_loop(0, blocks, finish, 0)


def encode(x_enc, enc_len, wq, wk, wv, wo, w1, w2, cwk, cwv):
    rows, seq, d = x_enc.shape
    layers, ff = w1.shape[0], w1.shape[2]
    heads = d // HD
    tokens = rows * seq + seq
    any_spec = pl.BlockSpec(memory_space=pl.ANY)
    big = pltpu.VMEM((tokens, d), BF)
    out = jax.ShapeDtypeStruct((layers, tokens, d), BF)
    return pl.pallas_call(
        functools.partial(encoder_kernel, rows, seq),
        out_shape=(out, out),
        in_specs=[pl.BlockSpec(memory_space=pltpu.SMEM)] + [any_spec] * 9,
        out_specs=(any_spec, any_spec),
        scratch_shapes=[big, big, big, big, big, pltpu.VMEM((BLK, ff), BF),
                        pltpu.VMEM((heads, HD + GRAN, seq), BF), pltpu.VMEM((d, seq), BF)]
        + [pltpu.VMEM(w.shape, BF) for w in (wq, wk, wv, wo, w1, w2, cwk, cwv)]
        + [pltpu.SMEM((rows,), jnp.int32), pltpu.SemaphoreType.DMA((rows,)), pltpu.SemaphoreType.DMA((layers, 8)),
           pltpu.SemaphoreType.DMA((4, tokens // BLK))],
        compiler_params=pltpu.CompilerParams(vmem_limit_bytes=60 * 1024 * 1024),
        cost_estimate=pl.CostEstimate(flops=60_000_000_000, bytes_accessed=40_000_000, transcendentals=0),
        name="encoder",
    )(enc_len, x_enc, wq, wk, wv, wo, w1, w2, cwk, cwv)


def decoder_kernel(rows, seq, per_block, len_ref, y_hbm, ck_hbm, cv_hbm, wq_h, wk_h, wv_h, wo_h, xq_h, xo_h, w1_h, w2_h, out_hbm,
                   z_ref, ck, cv, u_ref, vtx_ref, ctx_ref, cq_ref, cc_ref,
                   wq, wk, wv, wo, xq, xo, w1, w2, start_ref, y_sem, w_sem, k_sem, o_sem):
    layers = wq.shape[0]
    dec = y_hbm.shape[0] // rows
    heads = ctx_ref.shape[0] // HD
    y_copy = pltpu.make_async_copy(y_hbm, z_ref, y_sem)
    y_copy.start()
    starts = row_starts(len_ref, rows)
    for r in range(rows):
        start_ref[r] = starts[r]
    pairs = [(wq_h, wq), (wk_h, wk), (wv_h, wv), (wo_h, wo), (xq_h, xq), (xo_h, xo), (w1_h, w1), (w2_h, w2)]
    w_copies = {}

    def kv_copies(r, layer):
        at = pl.ds(pl.multiple_of(start_ref[r], GRAN), seq)
        return (pltpu.make_async_copy(ck_hbm.at[layer, at], ck.at[layer, r], k_sem.at[layer, 0, r]),
                pltpu.make_async_copy(cv_hbm.at[layer, at], cv.at[layer, r], k_sem.at[layer, 1, r]))

    for layer in range(layers):
        for i, (src, dst) in enumerate(pairs):
            w_copies[i, layer] = pltpu.make_async_copy(src.at[layer], dst.at[layer], w_sem.at[layer, i])
            if i < 6:
                w_copies[i, layer].start()
        for r in range(rows):
            for copy in kv_copies(r, layer):
                copy.start()
        for i in range(6, 8):
            w_copies[i, layer].start()
    y_copy.wait()

    m = per_block * dec
    ki = lax.broadcasted_iota(jnp.int32, (m, m), 0)
    qi = lax.broadcasted_iota(jnp.int32, (m, m), 1)
    causal = (ki <= qi) & (ki // dec == qi // dec)
    vtx_ref[:, HD:HD + GRAN, :] = jnp.ones((heads, GRAN, m), BF)
    lane = lax.broadcasted_iota(jnp.int32, (dec, heads * HD), 1)

    for layer in range(layers):
        for i in range(8):
            w_copies[i, layer].wait()

        def wait_row(r, carry):
            for copy in kv_copies(r, layer):
                copy.wait()
            return carry
        lax.fori_loop(0, rows, wait_row, 0)

        def block(b, carry):
            at = pl.ds(pl.multiple_of(b * m, m), m)
            z = z_ref[at]
            zn = norm(z)
            q = dot(zn, wq[layer]).astype(BF) * BF(HD ** -0.5)
            k = dot(zn, wk[layer]).astype(BF)
            v = dot(zn, wv[layer]).astype(BF)
            store_values(v, vtx_ref, m)
            head_attention(k, q, vtx_ref, ctx_ref, causal)
            z1 = (z.astype(F32) + dot(ctx_ref[...].T, wo[layer])).astype(BF)
            cq_ref[...] = dot(norm(z1), xq[layer]).astype(BF) * BF(HD ** -0.5)

            def cross(r, carry2):
                row = b * per_block + r
                length = len_ref[row]
                mine = pl.ds(pl.multiple_of(r * dec, dec), dec)
                qr = cq_ref[mine]
                qs = jnp.concatenate([jnp.where(lane // HD == h, qr, jnp.zeros((), BF)) for h in range(heads)], axis=0)
                s = dot_t(qs, ck[layer, row])
                s = jnp.where(lax.broadcasted_iota(jnp.int32, (1, seq), 1) < length, s, NEG)
                top = jnp.max(s, axis=1, keepdims=True)
                e = jnp.exp2((s - top) * LOG2E)
                p = (e * (1.0 / jnp.sum(e, axis=1, keepdims=True))).astype(BF)
                vals = jnp.where(lax.broadcasted_iota(jnp.int32, (seq, 1), 0) < length, cv[layer, row], jnp.zeros((), BF))
                o = dot(p, vals)
                first = lax.broadcasted_iota(jnp.int32, (dec, 2 * HD), 1) < HD
                for j in range(heads // 2):
                    cols = slice(128 * j, 128 * j + 128)
                    cc_ref[mine, cols] = jnp.where(first, o[2 * j * dec:(2 * j + 1) * dec, cols],
                                                   o[(2 * j + 1) * dec:(2 * j + 2) * dec, cols]).astype(BF)
                return carry2
            lax.fori_loop(0, per_block, cross, 0)
            z2 = (z1.astype(F32) + dot(cc_ref[...], xo[layer])).astype(BF)
            z_ref[at] = ffn(z2, w1, w2, layer, u_ref)
            return carry
        lax.fori_loop(0, rows // per_block, block, 0)

    out_copy = pltpu.make_async_copy(z_ref, out_hbm, o_sem)
    out_copy.start()
    out_copy.wait()


def decode(y, enc_len, ck, cv, seq, wq, wk, wv, wo, xq, xo, w1, w2):
    rows, dec, d = y.shape
    layers, ff = w1.shape[0], w1.shape[2]
    heads = d // HD
    per_block = BLK // dec
    any_spec = pl.BlockSpec(memory_space=pl.ANY)
    weights = (wq, wk, wv, wo, xq, xo, w1, w2)
    out = pl.pallas_call(
        functools.partial(decoder_kernel, rows, seq, per_block),
        out_shape=jax.ShapeDtypeStruct((rows * dec, d), BF),
        in_specs=[pl.BlockSpec(memory_space=pltpu.SMEM)] + [any_spec] * 11,
        out_specs=any_spec,
        scratch_shapes=[pltpu.VMEM((rows * dec, d), BF), pltpu.VMEM((layers, rows, seq, d), BF), pltpu.VMEM((layers, rows, seq, d), BF),
                        pltpu.VMEM((BLK, ff), BF), pltpu.VMEM((heads, HD + GRAN, BLK), BF), pltpu.VMEM((d, BLK), BF),
                        pltpu.VMEM((BLK, d), BF), pltpu.VMEM((BLK, d), BF)]
        + [pltpu.VMEM(w.shape, BF) for w in weights]
        + [pltpu.SMEM((rows,), jnp.int32), pltpu.SemaphoreType.DMA, pltpu.SemaphoreType.DMA((layers, 8)),
           pltpu.SemaphoreType.DMA((layers, 2, rows)), pltpu.SemaphoreType.DMA],
        compiler_params=pltpu.CompilerParams(vmem_limit_bytes=60 * 1024 * 1024),
        cost_estimate=pl.CostEstimate(flops=12_000_000_000, bytes_accessed=40_000_000, transcendentals=0),
        name="decoder",
    )(enc_len, y.reshape(rows * dec, d), ck, cv, *weights)
    return out.reshape(rows, dec, d)


def solution(mesh):
    pair_size = mesh.shape["pair"]
    to_partner = [(source, (source + pair_size // 2) % pair_size) for source in range(pair_size)]
    row_spec = P(("data", "pair"))
    full_spec = P()

    def per_device(x_enc, enc_len, y_dec, enc_wq, enc_wk, enc_wv, enc_wo, enc_w1, enc_w2, dec_wq, dec_wk, dec_wv, dec_wo, crs_wq, crs_wk, crs_wv, crs_wo, dec_w1, dec_w2):
        d = x_enc.shape[2]
        flat = lambda w: w.reshape(w.shape[0], w.shape[1] * w.shape[2], d)
        y_here = lax.ppermute(y_dec, "pair", to_partner)
        ck, cv = encode(x_enc, enc_len, enc_wq, enc_wk, enc_wv, flat(enc_wo), enc_w1, enc_w2, crs_wk, crs_wv)
        out_here = decode(y_here, enc_len, ck, cv, x_enc.shape[1], dec_wq, dec_wk, dec_wv, flat(dec_wo), crs_wq, flat(crs_wo), dec_w1, dec_w2)
        return lax.ppermute(out_here, "pair", to_partner)

    return jax.shard_map(per_device, mesh=mesh, in_specs=(row_spec, row_spec, row_spec) + (full_spec,) * 16, out_specs=row_spec, check_vma=False)
```

time: 642 us -> 233 us (0.36)
  the two profiles are of different devices: /device:TPU:0 before, /device:TPU:31 now
where the time goes in v1:
time: 233 us; the launch traced here: 236 us
  Pallas kernels  192 us (82%)
  starting transfers between devices  35.2 us (15%)
  waiting for transfers between devices  6.57 us (3%)
    pallas_call x1, Pallas kernels, encode(): pl.pallas_call(functools.partial(encoder_kernel, rows, seq), out_shape=(o...  136 us
    pallas_call x1, Pallas kernels, decode(): pl.pallas_call(functools.partial(decoder_kernel, rows, seq, per_block), o...  56.6 us
    ppermute x1, starting transfers between devices, per_device(): return lax.ppermute(out_here, 'pair', to_partner)  31.6 us
    ppermute x1, waiting for transfers between devices, per_device(): return lax.ppermute(out_here, 'pair', to_partner)  6.57 us
  transfers between devices with their start and end apart: 2, of which 1 were waited for; matrix products, arithmetic and copies ran while one was open for 0% of the time, Pallas kernels for 58%

profile of v1, /device:TPU:31, one launch (start us, length us, event | category | flops | bytes accessed | tf_op | source)
XLA Modules:
  0.0 235.8 jit_solution(6097314346266153566)
XLA Ops:
  0.0 3.6 %collective-permute-start = (bf16[16,32,512]{2,1,0:T(8,128)(2,1)}, bf16[16,32,512]{2,1,0:T(8,128)(2,1)S(1)}, u32[]{:S(2)}, u32[]{:S(2)}) collective-permute-start(bf16[16,32,512]{2,1,0:T(8,128)(2,1)} %param.21), channel_id=1, source_target_pairs={{0,64},{1,65},{2,66},{3,67},{4,68},{5,69},{6,70},{7,71},{8,72},{9,... | collective-permute-start | bytes 1572872 | tf_op jit(solution)/shard_map/ppermute | solution.py:326
  3.6 135.8 %encoder.1 = (bf16[2,4352,512]{2,1,0:T(8,128)(2,1)}, bf16[2,4352,512]{2,1,0:T(8,128)(2,1)}) custom-call(s32[16]{0:T(128)} %len_ref.3, bf16[16,256,512]{2,1,0:T(8,128)(2,1)} %x_hbm.1, bf16[2,512,512]{2,1,0:T(8,128)(2,1)} %wq_h.2, bf16[2,512,512]{2,1,0:T(8,128)(2,1)} %wk_h.2, bf16[2,512,512]{2,1,0:T(8,128)(2,1)} %wv_h.2, bf16[2,512,512]{2,1,0:T(8,128)(2,1)} %bitcast.5, ...), custom_call_target="tpu_custom_call" | custom-call | flops 60000002048 | bytes 40000000 | tf_op jit(solution)/shard_map/encoder/pallas_call | solution.py:186
  139.4 0.0 collective-permute-done
  139.4 0.0 copy-start
  139.4 0.8 copy-done
  140.2 56.6 %decoder.1 = bf16[512,512]{1,0:T(8,128)(2,1)} custom-call(s32[16]{0:T(128)} %len_ref.3, bf16[512,512]{1,0:T(8,128)(2,1)} %bitcast.8, bf16[2,4352,512]{2,1,0:T(8,128)(2,1)} %get-tuple-element.7.ck_hbm, bf16[2,4352,512]{2,1,0:T(8,128)(2,1)} %get-tuple-element.8.cv_hbm, bf16[2,512,512]{2,1,0:T(8,128)(2,1)} %wq_h.3, bf16[2,512,512]{2,1,0:T(8,128)(2,1)} %wk_h.3, ...), custom_call_target="tpu_custom_call" | custom-call | flops 12000000000 | bytes 40000000 | tf_op jit(solution)/shard_map/decoder/pallas_call | solution.py:299
  196.8 31.6 %collective-permute-start.1 = (bf16[16,32,512]{2,1,0:T(8,128)(2,1)}, bf16[16,32,512]{2,1,0:T(8,128)(2,1)S(1)}, u32[]{:S(2)}, u32[]{:S(2)}) collective-permute-start(bf16[16,32,512]{2,1,0:T(8,128)(2,1)} %bitcast.9), channel_id=1, source_target_pairs={{0,64},{1,65},{2,66},{3,67},{4,68},{5,69},{6,70},{7,71},{8,72},{9,... | collective-permute-start | bytes 1572872 | tf_op jit(solution)/shard_map/ppermute | solution.py:329
  228.4 6.6 %collective-permute-done.1 = bf16[16,32,512]{2,1,0:T(8,128)(2,1)S(1)} collective-permute-done((bf16[16,32,512]{2,1,0:T(8,128)(2,1)}, bf16[16,32,512]{2,1,0:T(8,128)(2,1)S(1)}, u32[]{:S(2)}, u32[]{:S(2)}) %collective-permute-start.1) | collective-permute-done | bytes 524320 | tf_op jit(solution)/shard_map/ppermute | solution.py:329
  235.0 0.8 copy.21
Async XLA Ops:
  0.0 139.4 %collective-permute-start = (bf16[16,32,512]{2,1,0:T(8,128)(2,1)}, bf16[16,32,512]{2,1,0:T(8,128)(2,1)S(1)}, u32[]{:S(2)}, u32[]{:S(2)}) collective-permute-start(bf16[16,32,512]{2,1,0:T(8,128)(2,1)} %param.21), channel_id=1, source_target_pairs={{0,64},{1,65},{2,66},{3,67},{4,68},{5,69},{6,70},{7,71},{8,72},{9,... | collective-permute-start | bytes 1572872 | tf_op jit(solution)/shard_map/ppermute | solution.py:326
  139.4 0.8 copy-start
  196.8 38.2 %collective-permute-start.1 = (bf16[16,32,512]{2,1,0:T(8,128)(2,1)}, bf16[16,32,512]{2,1,0:T(8,128)(2,1)S(1)}, u32[]{:S(2)}, u32[]{:S(2)}) collective-permute-start(bf16[16,32,512]{2,1,0:T(8,128)(2,1)} %bitcast.9), channel_id=1, source_target_pairs={{0,64},{1,65},{2,66},{3,67},{4,68},{5,69},{6,70},{7,71},{8,72},{9,... | collective-permute-start | bytes 1572872 | tf_op jit(solution)/shard_map/ppermute | solution.py:329
